TPU v7x, 256 devices: a whole 4x4x8 slice. The times are simulated.
256 devices in a mesh: ep: 8 (over y, core), fsdp: 32 (over z, x).
Axes of the slice: x: 4, y: 4, z: 8, core: 2. Of those that a mesh axis runs over, the one named last changes fastest.
Arguments:
- w_down: float32 [16, 6400, 4096], P('ep', None, 'fsdp'), may hold values from -0.15625 to 0.15625
- router_weight: float32 [4096, 16], P('fsdp', 'ep'), may hold values from -0.09375 to 0.09375
- router_gain: float32 [4096], P('fsdp'), may hold values from 0.25 to 1.75
Outputs:
- serve_down: bfloat16 [16, 6400, 4096], P('ep', 'fsdp')
- scale_down: float32 [16, 6400], P('ep', 'fsdp')
- serve_router: bfloat16 [4096, 16], replicated
All inputs are finite; a program needn't handle non-finite values.
Results may differ from a plain program's by a relative error of at most 0.001.
Values may be sent and summed in bfloat16 or wider, within the bound.
A program may use at most 64 MiB of HBM per device.

v0:
```python
import jax
import jax.numpy as jnp
from jax import lax
from jax.sharding import Mesh
from jax.sharding import PartitionSpec as P

FSDP = ("fsdp_0", "fsdp_1")


def by_axis(array, axes):
    for axis in axes:
        array = lax.psum(array, axis)
    return array


def in_order(parts, dim):
    lengths = list(parts.shape[1:])
    lengths[dim] *= parts.shape[0]
    return jnp.moveaxis(parts, 0, dim).reshape(lengths)


def copy_for_each(array, axis):
    size = lax.axis_size(axis)
    return lax.all_to_all(
        jnp.broadcast_to(array[None], (size, *array.shape)), axis, 0, 0, tiled=True
    )


def gather_directly(array, axis, dim):
    return in_order(copy_for_each(array, axis), dim)


def body(w_down, router_weight, router_gain):
    total_down = by_axis(jnp.sum(w_down * w_down, axis=2), FSDP)
    scale_down = jnp.sqrt(total_down)
    narrow_down = (w_down / jnp.expand_dims(scale_down, 2)).astype(jnp.bfloat16)
    serve_down = lax.all_to_all(narrow_down, FSDP, split_axis=1, concat_axis=2, tiled=True)
    scale_down = lax.dynamic_slice_in_dim(
        scale_down, lax.axis_index(FSDP) * serve_down.shape[1], serve_down.shape[1], axis=1
    )
    part_router = (router_weight * router_gain[:, None]).astype(jnp.bfloat16)
    row_router = gather_directly(part_router, FSDP, 0)
    serve_router = lax.all_gather(row_router, "ep", axis=1, tiled=True)
    return (serve_down, scale_down, serve_router)


def solution(mesh):
    split = Mesh(mesh.devices.reshape(mesh.shape["ep"], 8, 4), ("ep", "fsdp_0", "fsdp_1"))
    return jax.shard_map(
        body,
        mesh=split,
        in_specs=(P("ep", None, FSDP), P(FSDP, "ep"), P(FSDP)),
        out_specs=(P("ep", FSDP, None), P("ep", FSDP), P()),
        check_vma=False,
    )
```

profile of v0, /device:TPU:8, one launch (start us, length us, event | category | flops | bytes accessed | tf_op | source)
XLA Modules:
  0.0 177.8 jit_solution(15432574918795712005)
XLA Ops:
  0.6 0.7 multiply_convert_fusion
  1.3 0.6 broadcast_in_dim.2
  1.9 11.3 %all-to-all-start.1 = ((bf16[32,128,2]{1,2,0:T(2,128)(2,1)}), bf16[32,128,2]{1,2,0:T(2,128)(2,1)S(1)}, u32[]{:S(2)}, u32[]{:S(2)}) async-start(bf16[32,128,2]{1,2,0:T(2,128)(2,1)} %broadcast_in_dim.2), calls=%async_computation.1 | async-start | bytes 32768 | tf_op jit(solution)/shard_map/all_to_all | solution.py:24
  13.3 4.6 %multiply_reduce_fusion = f32[2,6400]{1,0:T(2,128)S(1)} fusion(f32[2,6400,128]{2,1,0:T(8,128)} %param.3), kind=kLoop, calls=%fused_computation.1 | loop fusion | flops 3264000 | bytes 6604800 | tf_op jit(solution)/shard_map/reduce_sum | solution.py:34
  17.9 30.5 %psum.14 = f32[2,6400]{1,0:T(2,128)S(1)} all-reduce(f32[2,6400]{1,0:T(2,128)S(1)} %multiply_reduce_fusion), channel_id=1, replica_groups=mesh['ep'=8,'fsdp_0'=8,'fsdp_1'=4] {'fsdp_0'}, use_global_device_ids=true, to_apply=%region_1.0 | all-reduce | flops 12800 | bytes 102400 | tf_op jit(solution)/shard_map/psum | solution.py:12
  48.4 17.4 %psum.15 = f32[2,6400]{1,0:T(2,128)S(1)} all-reduce(f32[2,6400]{1,0:T(2,128)S(1)} %psum.14), channel_id=1, replica_groups=mesh['ep'=8,'fsdp_0'=8,'fsdp_1'=4] {'fsdp_1'}, use_global_device_ids=true, to_apply=%region_2.0 | all-reduce | flops 12800 | bytes 102400 | tf_op jit(solution)/shard_map/psum | solution.py:12
  65.8 0.1 sqrt.3
  65.9 4.7 %divide_convert_fusion = bf16[2,6400,128]{2,1,0:T(8,128)(2,1)S(1)} fusion(f32[2,6400,128]{2,1,0:T(8,128)} %param.3, f32[2,6400]{1,0:T(2,128)S(1)} %sqrt.3), kind=kLoop, calls=%fused_computation | loop fusion | flops 3276800 | bytes 9881600 | tf_op jit(solution)/shard_map/convert_element_type | solution.py:36
  70.6 27.9 %copy.10 = bf16[2,6400,128]{2,0,1:T(2,128)(2,1)} copy(bf16[2,6400,128]{2,1,0:T(8,128)(2,1)S(1)} %divide_convert_fusion) | data formatting | bytes 6553600 | tf_op jit(solution)/shard_map/convert_element_type | solution.py:36
  98.5 0.0 all-to-all-done.1
  98.5 5.7 %all-to-all-start = ((bf16[2,6400,128]{2,0,1:T(2,128)(2,1)}), bf16[2,6400,128]{2,0,1:T(2,128)(2,1)S(1)}, u32[]{:S(2)}, u32[]{:S(2)}) async-start(bf16[2,6400,128]{2,0,1:T(2,128)(2,1)} %copy.10), calls=%async_computation | async-start | bytes 6553600 | tf_op jit(solution)/shard_map/all_to_all | solution.py:37
  104.2 0.7 constant_dynamic-slice_fusion
  104.9 12.9 %all-gather = bf16[8,2,4096]{2,1,0:T(2,128)(2,1)S(1)} all-gather(bf16[1,2,4096]{2,1,0:T(2,128)(2,1)S(1)} %bitcast.13), channel_id=1, replica_groups=mesh['ep'=8,'fsdp_0'=8,'fsdp_1'=4] {'ep'}, dimensions={0}, use_global_device_ids=true | all-gather | bytes 147456 | tf_op jit(solution)/shard_map/all_gather | solution.py:43
  117.8 0.7 reshape.14
  118.5 50.5 %all-to-all-done = bf16[2,6400,128]{2,0,1:T(2,128)(2,1)S(1)} async-done(((bf16[2,6400,128]{2,0,1:T(2,128)(2,1)}), bf16[2,6400,128]{2,0,1:T(2,128)(2,1)S(1)}, u32[]{:S(2)}, u32[]{:S(2)}) %all-to-all-start) | async-done | bytes 3276832 | tf_op jit(solution)/shard_map/all_to_all | solution.py:37
  169.1 2.5 %copy.11 = bf16[2,200,32,128]{3,2,1,0:T(8,128)(2,1)} copy(bf16[2,200,32,128]{3,0,1,2:T(2,128)(2,1)S(1)} %bitcast.11) | data formatting | bytes 6553600 | tf_op jit(solution)/shard_map/all_to_all | solution.py:37
  171.6 6.2 %all_to_all.19 = bf16[2,200,4096]{2,1,0:T(8,128)(2,1)} reshape(bf16[2,200,32,128]{3,2,1,0:T(8,128)(2,1)} %copy.11) | data formatting | bytes 6553600 | tf_op jit(solution)/shard_map/all_to_all | solution.py:37
Async XLA Ops:
  1.9 96.6 %all-to-all-start.1 = ((bf16[32,128,2]{1,2,0:T(2,128)(2,1)}), bf16[32,128,2]{1,2,0:T(2,128)(2,1)S(1)}, u32[]{:S(2)}, u32[]{:S(2)}) async-start(bf16[32,128,2]{1,2,0:T(2,128)(2,1)} %broadcast_in_dim.2), calls=%async_computation.1 | async-start | bytes 32768 | tf_op jit(solution)/shard_map/all_to_all | solution.py:24
  98.5 70.6 %all-to-all-start = ((bf16[2,6400,128]{2,0,1:T(2,128)(2,1)}), bf16[2,6400,128]{2,0,1:T(2,128)(2,1)S(1)}, u32[]{:S(2)}, u32[]{:S(2)}) async-start(bf16[2,6400,128]{2,0,1:T(2,128)(2,1)} %copy.10), calls=%async_computation | async-start | bytes 6553600 | tf_op jit(solution)/shard_map/all_to_all | solution.py:37
where the time goes:
time: 178 us
  blocking collectives  60.9 us (34%)
  waiting for transfers between devices  50.5 us (28%)
  local copies, waits for them, and re-layouts  38.6 us (22%)
  starting transfers between devices  17 us (10%)
  other arithmetic  10 us (6%)
    all_to_all x1, waiting for transfers between devices, body(): lax.all_to_all(narrow_down, FSDP, split_axis=1, concat_axis=2, tiled=True)  50.5 us
    psum x2, blocking collectives, by_axis(): array = lax.psum(array, axis)  47.9 us
    convert_element_type x1, local copies, waits for them, and re-layouts, body(): narrow_down = (w_down / jnp.expand_dims(scale_down, 2)).astype(jnp.bfloat16)  27.9 us
    all_gather x1, blocking collectives, body(): serve_router = lax.all_gather(row_router, 'ep', axis=1, tiled=True)  12.9 us
    all_to_all x1, starting transfers between devices, copy_for_each(): lax.all_to_all(jnp.broadcast_to(array[None], (size, *array.shape)), axis,...  11.3 us
    all_to_all x2, local copies, waits for them, and re-layouts, body(): lax.all_to_all(narrow_down, FSDP, split_axis=1, concat_axis=2, tiled=True)  8.73 us
    all_to_all x1, starting transfers between devices, body(): lax.all_to_all(narrow_down, FSDP, split_axis=1, concat_axis=2, tiled=True)  5.7 us
    convert_element_type x1, other arithmetic, body(): narrow_down = (w_down / jnp.expand_dims(scale_down, 2)).astype(jnp.bfloat16)  4.71 us
  transfers between devices with their start and end apart: 2, of which 1 were waited for; matrix products, arithmetic and copies ran while one was open for 22% of the time, Pallas kernels for 0%

commit v1 on v0

--- a/solution.py
+++ b/solution.py
@@ -40,7 +40,9 @@
     )
     part_router = (router_weight * router_gain[:, None]).astype(jnp.bfloat16)
     row_router = gather_directly(part_router, FSDP, 0)
-    serve_router = lax.all_gather(row_router, "ep", axis=1, tiled=True)
+    serve_router = jnp.concatenate(
+        lax.all_to_all(jnp.stack([row_router] * lax.axis_size("ep")), "ep", 0, 0), axis=1
+    )
     return (serve_down, scale_down, serve_router)
 
 

time: 178 us -> 197 us (1.11); the launches traced: 178 us -> 194 us
  waiting for transfers between devices: 50.5 us -> 73.9 us
  blocking collectives: 60.9 us -> 47.9 us
  starting transfers between devices: 17 us -> 21.9 us
    all_to_all x1, waiting for transfers between devices: 50.5 us -> 73.9 us  [body(): lax.all_to_all(narrow_down, FSDP, split_axis=1, concat_axis=2, tiled=True)]
    all_gather x1 -> x0, blocking collectives: 12.9 us -> none  [body(): serve_router = lax.all_gather(row_router, 'ep', axis=1, tiled=True)]
    all_to_all x0 -> x1, starting transfers between devices: none -> 4.92 us  [body(): lax.all_to_all(jnp.stack([row_router] * lax.axis_size('ep')), 'ep', 0, 0)]
  transfers between devices with their start and end apart: 2 -> 3, of which waited for: 1 -> 1; matrix products, arithmetic and copies ran while one was open for 22% -> 20% of each run, Pallas kernels for 0% -> 0%
where the time goes in v1:
time: 197 us; the launch traced here: 194 us
  waiting for transfers between devices  73.9 us (38%)
  blocking collectives  47.9 us (24%)
  local copies, waits for them, and re-layouts  39.4 us (20%)
  starting transfers between devices  21.9 us (11%)
  other arithmetic  10 us (5%)
    all_to_all x1, waiting for transfers between devices, body(): lax.all_to_all(narrow_down, FSDP, split_axis=1, concat_axis=2, tiled=True)  73.9 us
    psum x2, blocking collectives, by_axis(): array = lax.psum(array, axis)  47.9 us
    convert_element_type x1, local copies, waits for them, and re-layouts, body(): narrow_down = (w_down / jnp.expand_dims(scale_down, 2)).astype(jnp.bfloat16)  27.9 us
    all_to_all x1, starting transfers between devices, copy_for_each(): lax.all_to_all(jnp.broadcast_to(array[None], (size, *array.shape)), axis,...  11.3 us
    all_to_all x2, local copies, waits for them, and re-layouts, body(): lax.all_to_all(narrow_down, FSDP, split_axis=1, concat_axis=2, tiled=True)  8.73 us
    all_to_all x1, starting transfers between devices, body(): lax.all_to_all(narrow_down, FSDP, split_axis=1, concat_axis=2, tiled=True)  5.7 us
    all_to_all x1, starting transfers between devices, body(): lax.all_to_all(jnp.stack([row_router] * lax.axis_size('ep')), 'ep', 0, 0)  4.92 us
    convert_element_type x1, other arithmetic, body(): narrow_down = (w_down / jnp.expand_dims(scale_down, 2)).astype(jnp.bfloat16)  4.7 us
  transfers between devices with their start and end apart: 3, of which 1 were waited for; matrix products, arithmetic and copies ran while one was open for 20% of the time, Pallas kernels for 0%

profile of v1, /device:TPU:8, one launch (start us, length us, event | category | flops | bytes accessed | tf_op | source)
XLA Modules:
  0.0 193.8 jit_solution(6161485286738521264)
XLA Ops:
  0.6 0.7 multiply_convert_fusion
  1.3 0.6 broadcast_in_dim.2
  1.9 11.3 %all-to-all-start.1 = ((bf16[32,128,2]{1,2,0:T(2,128)(2,1)}), bf16[32,128,2]{1,2,0:T(2,128)(2,1)S(1)}, u32[]{:S(2)}, u32[]{:S(2)}) async-start(bf16[32,128,2]{1,2,0:T(2,128)(2,1)} %broadcast_in_dim.2), calls=%async_computation.1 | async-start | bytes 32768 | tf_op jit(solution)/shard_map/all_to_all | solution.py:24
  13.3 4.6 %multiply_reduce_fusion = f32[2,6400]{1,0:T(2,128)S(1)} fusion(f32[2,6400,128]{2,1,0:T(8,128)} %param.3), kind=kLoop, calls=%fused_computation.1 | loop fusion | flops 3264000 | bytes 6604800 | tf_op jit(solution)/shard_map/reduce_sum | solution.py:34
  17.9 30.5 %psum.14 = f32[2,6400]{1,0:T(2,128)S(1)} all-reduce(f32[2,6400]{1,0:T(2,128)S(1)} %multiply_reduce_fusion), channel_id=1, replica_groups=mesh['ep'=8,'fsdp_0'=8,'fsdp_1'=4] {'fsdp_0'}, use_global_device_ids=true, to_apply=%region_1.0 | all-reduce | flops 12800 | bytes 102400 | tf_op jit(solution)/shard_map/psum | solution.py:12
  48.4 17.4 %psum.15 = f32[2,6400]{1,0:T(2,128)S(1)} all-reduce(f32[2,6400]{1,0:T(2,128)S(1)} %psum.14), channel_id=1, replica_groups=mesh['ep'=8,'fsdp_0'=8,'fsdp_1'=4] {'fsdp_1'}, use_global_device_ids=true, to_apply=%region_2.0 | all-reduce | flops 12800 | bytes 102400 | tf_op jit(solution)/shard_map/psum | solution.py:12
  65.8 0.1 sqrt.3
  65.9 0.0 all-to-all-done.1
  65.9 0.7 stack.3
  66.6 4.9 %all-to-all-start.2 = ((bf16[8,4096,2]{1,2,0:T(2,128)(2,1)}), bf16[8,4096,2]{1,2,0:T(2,128)(2,1)S(1)}, u32[]{:S(2)}, u32[]{:S(2)}) async-start(bf16[8,4096,2]{1,2,0:T(2,128)(2,1)} %stack.3), calls=%async_computation.2 | async-start | bytes 262144 | tf_op jit(solution)/shard_map/all_to_all | solution.py:44
  71.6 4.7 %divide_convert_fusion = bf16[2,6400,128]{2,1,0:T(8,128)(2,1)S(1)} fusion(f32[2,6400,128]{2,1,0:T(8,128)} %param.3, f32[2,6400]{1,0:T(2,128)S(1)} %sqrt.3), kind=kLoop, calls=%fused_computation | loop fusion | flops 3276800 | bytes 9881600 | tf_op jit(solution)/shard_map/convert_element_type | solution.py:36
  76.3 27.9 %copy.10 = bf16[2,6400,128]{2,0,1:T(2,128)(2,1)} copy(bf16[2,6400,128]{2,1,0:T(8,128)(2,1)S(1)} %divide_convert_fusion) | data formatting | bytes 6553600 | tf_op jit(solution)/shard_map/convert_element_type | solution.py:36
  104.1 0.0 all-to-all-done.2
  104.1 5.7 %all-to-all-start = ((bf16[2,6400,128]{2,0,1:T(2,128)(2,1)}), bf16[2,6400,128]{2,0,1:T(2,128)(2,1)S(1)}, u32[]{:S(2)}, u32[]{:S(2)}) async-start(bf16[2,6400,128]{2,0,1:T(2,128)(2,1)} %copy.10), calls=%async_computation | async-start | bytes 6553600 | tf_op jit(solution)/shard_map/all_to_all | solution.py:37
  109.9 0.7 constant_dynamic-slice_fusion
  110.5 0.7 reshape.18
  111.2 73.9 %all-to-all-done = bf16[2,6400,128]{2,0,1:T(2,128)(2,1)S(1)} async-done(((bf16[2,6400,128]{2,0,1:T(2,128)(2,1)}), bf16[2,6400,128]{2,0,1:T(2,128)(2,1)S(1)}, u32[]{:S(2)}, u32[]{:S(2)}) %all-to-all-start) | async-done | bytes 3276832 | tf_op jit(solution)/shard_map/all_to_all | solution.py:37
  185.1 2.5 %copy.11 = bf16[2,200,32,128]{3,2,1,0:T(8,128)(2,1)} copy(bf16[2,200,32,128]{3,0,1,2:T(2,128)(2,1)S(1)} %bitcast.9) | data formatting | bytes 6553600 | tf_op jit(solution)/shard_map/all_to_all | solution.py:37
  187.6 6.2 %all_to_all.22 = bf16[2,200,4096]{2,1,0:T(8,128)(2,1)} reshape(bf16[2,200,32,128]{3,2,1,0:T(8,128)(2,1)} %copy.11) | data formatting | bytes 6553600 | tf_op jit(solution)/shard_map/all_to_all | solution.py:37
Async XLA Ops:
  1.9 64.0 %all-to-all-start.1 = ((bf16[32,128,2]{1,2,0:T(2,128)(2,1)}), bf16[32,128,2]{1,2,0:T(2,128)(2,1)S(1)}, u32[]{:S(2)}, u32[]{:S(2)}) async-start(bf16[32,128,2]{1,2,0:T(2,128)(2,1)} %broadcast_in_dim.2), calls=%async_computation.1 | async-start | bytes 32768 | tf_op jit(solution)/shard_map/all_to_all | solution.py:24
  66.6 37.5 %all-to-all-start.2 = ((bf16[8,4096,2]{1,2,0:T(2,128)(2,1)}), bf16[8,4096,2]{1,2,0:T(2,128)(2,1)S(1)}, u32[]{:S(2)}, u32[]{:S(2)}) async-start(bf16[8,4096,2]{1,2,0:T(2,128)(2,1)} %stack.3), calls=%async_computation.2 | async-start | bytes 262144 | tf_op jit(solution)/shard_map/all_to_all | solution.py:44
  104.1 81.0 %all-to-all-start = ((bf16[2,6400,128]{2,0,1:T(2,128)(2,1)}), bf16[2,6400,128]{2,0,1:T(2,128)(2,1)S(1)}, u32[]{:S(2)}, u32[]{:S(2)}) async-start(bf16[2,6400,128]{2,0,1:T(2,128)(2,1)} %copy.10), calls=%async_computation | async-start | bytes 6553600 | tf_op jit(solution)/shard_map/all_to_all | solution.py:37
